TPU v7x, 32 devices: a whole 2x2x4 slice. The times are simulated.
32 devices in a mesh: row: 8 (over z, core), col: 2 (over x), gz: 2 (over y).
Axes of the slice: x: 2, y: 2, z: 4, core: 2. Of those that a mesh axis runs over, the one named last changes fastest.
Arguments:
- initial_field: float32 [8, 32, 32, 256], P(None, 'row', 'col', 'gz'), may hold values from -6 to 6
- source_term: float32 [8, 32, 32, 256], P(None, 'row', 'col', 'gz'), may hold values from -6 to 6
- cell_class: int32 [32, 32, 256], P('row', 'col', 'gz'), may hold values from 0 to 15
- class_shift: float32 [16], replicated, may hold values from 0.05 to 4
- surface_cell: int32 [4096], P(('row', 'col', 'gz')), may hold values from 0 to 8191
- live_count: int32 [32], P(('row', 'col', 'gz')), may hold values from 1 to 128, 2560 in all
- panel_geometry: float32 [4, 4096], P(None, ('row', 'col', 'gz')), may hold values from 0.5 to 2
Outputs:
- final_field: float32 [8, 32, 32, 256], P(None, 'row', 'col', 'gz')
- boundary_potential: float32 [8, 4096], P(None, ('row', 'col', 'gz'))
Inputs may be any that keep to these rules, and one draw needn't show every extreme that they name: Slots 0 to live_count[b] - 1 of brick b are in use; the counts sum to 2560. `surface_cell`: A cell index inside the panel's own brick, x * 16 * 128 + y * 128 + z.
All inputs are finite; a program needn't handle non-finite values. No bound on the sum of `live_count` on one device may be relied on, other than what follows from the above.
Results may differ from a plain program's by a relative error of at most 0.004.
Values may be sent and summed in bfloat16 or wider, within the bound.
A program may use at most 128 MiB of HBM per device.

v0:
```python
import math

import jax
import jax.numpy as jnp
from jax import lax
from jax.sharding import PartitionSpec as P

SWEEPS = 3
ROUNDS = 2


relax_weight = 0.8
wave_number = 25.0
soften = 0.05
coupling = 0.5


def with_halo(x, sides, width):
    for axis, dim in sides:
        devices, length = (lax.axis_size(axis), x.shape[dim])
        up = [(i, (i + 1) % devices) for i in range(devices - 1)]
        down = [(j, i) for i, j in up]
        last = lax.slice_in_dim(x, length - width, length, axis=dim)
        initial = lax.slice_in_dim(x, 0, width, axis=dim)
        before = lax.ppermute(last, axis, up)
        after = lax.ppermute(initial, axis, down)
        x = jnp.concatenate([before, x, after], axis=dim)
    return x


def neighbours(padded):
    total = padded[:, 2:, 1:-1, 1:-1] + padded[:, :-2, 1:-1, 1:-1]
    total = total + padded[:, 1:-1, 2:, 1:-1] + padded[:, 1:-1, :-2, 1:-1]
    total = total + padded[:, 1:-1, 1:-1, 2:] + padded[:, 1:-1, 1:-1, :-2]
    return total


def relax(state, padded, forcing, shift_field):
    diagonal = 6.0 + shift_field
    residual = forcing - (diagonal * state - neighbours(padded))
    return state + relax_weight * residual / diagonal


def kernel_tile(sources, targets, factor):
    delta_x = targets[0][None, :] - sources[0][:, None]
    delta_y = targets[1][None, :] - sources[1][:, None]
    delta_z = targets[2][None, :] - sources[2][:, None]
    distance = jnp.sqrt(delta_x * delta_x + delta_y * delta_y + delta_z * delta_z)
    values = sources[3][:, None] * jnp.cos(wave_number * distance) / (distance + soften)
    return (values * factor).astype(jnp.bfloat16)


def shift_lookup(cell_class, class_shift):
    shift_field = jnp.zeros(cell_class.shape, jnp.float32)
    for level in range(class_shift.shape[0]):
        shift_field = shift_field + jnp.where(cell_class == level, class_shift[level], 0.0)
    return shift_field


def local(
    initial_field, source_term, cell_class, class_shift, surface_cell, live_count, panel_geometry
):
    channels, size_x, size_y, size_z = initial_field.shape
    slots = surface_cell.shape[0]
    panels = slots * lax.axis_size("row") * lax.axis_size("col") * lax.axis_size("gz")
    factor = 1.0 / math.sqrt(panels)
    shift_field = shift_lookup(cell_class, class_shift)
    live = (jnp.arange(slots, dtype=jnp.int32) < live_count[0]).astype(jnp.float32)
    source_geo = lax.all_gather(panel_geometry, ("row", "gz"), axis=1, tiled=True)
    target_geo = lax.all_gather(panel_geometry, "col", axis=1, tiled=True)
    state = initial_field
    load = jnp.zeros_like(source_term)
    potential = jnp.zeros((channels, slots), jnp.float32)
    for round_index in range(ROUNDS):
        forcing = source_term + load
        for sweep_index in range(SWEEPS):
            padded = with_halo(state, (("row", 1), ("col", 2), ("gz", 3)), 1)
            state = relax(state, padded, forcing, shift_field)
        density = (jnp.take(state.reshape(channels, -1), surface_cell, axis=1) * live).astype(
            jnp.bfloat16
        )
        initial = jnp.zeros((channels, target_geo.shape[1]), jnp.float32)
        piece = lax.all_gather(density, ("row", "gz"), axis=1, tiled=True)
        count = piece.shape[1]
        width = math.gcd(count, 512)

        def add_block(block_index, carry):
            offset = block_index * width
            values = lax.dynamic_slice_in_dim(piece, offset, width, 1)
            sources = lax.dynamic_slice_in_dim(source_geo, offset, width, 1)
            tile = kernel_tile(sources, target_geo, factor)
            return carry + jnp.dot(values, tile, preferred_element_type=jnp.float32)

        partial_value = lax.fori_loop(0, count // width, add_block, initial)
        summed = lax.psum_scatter(partial_value, "col", scatter_dimension=1, tiled=True)
        potential = summed * live
        if round_index + 1 < ROUNDS:
            spread = (
                jnp.zeros((channels, size_x * size_y * size_z), jnp.float32)
                .at[:, surface_cell]
                .add(coupling * potential)
            )
            load = spread.reshape(source_term.shape)
    return (state, potential)


def solution(mesh):
    placed = (
        P(None, "row", "col", "gz"),
        P(None, "row", "col", "gz"),
        P("row", "col", "gz"),
        P(),
        P(("row", "col", "gz")),
        P(("row", "col", "gz")),
        P(None, ("row", "col", "gz")),
    )
    return jax.shard_map(
        local,
        mesh=mesh,
        in_specs=placed,
        out_specs=(P(None, "row", "col", "gz"), P(None, ("row", "col", "gz"))),
        check_vma=False,
    )
```

profile of v0, /device:TPU:0, one launch (start us, length us, event | category | flops | bytes accessed | tf_op | source)
XLA Modules:
  0.0 312.9 jit_solution(12640101255865295727)
XLA Ops:
  12.9 3.0 collective-permute-done
  17.3 4.5 %collective-permute-start.3 = (f32[8,6,1,128]{3,0,2,1:T(8,128)S(1)}, f32[8,6,1,128]{3,0,2,1:T(8,128)S(1)}, u32[]{:S(2)}, u32[]{:S(2)}) collective-permute-start(f32[8,6,1,128]{3,0,2,1:T(8,128)S(1)} %copy.403), channel_id=1, source_target_pairs={{0,2},{1,3},{4,6},{5,7},{8,10},{9,11},{12,14},{13,15},{16,18},{17,... | collective-permute-start | bytes 73736 | tf_op jit(solution)/shard_map/ppermute | solution.py:25
  26.3 4.5 %collective-permute-start.5 = (f32[8,6,18,1]{2,0,3,1:T(8,128)S(1)}, f32[8,6,18,1]{2,0,3,1:T(8,128)S(1)}, u32[]{:S(2)}, u32[]{:S(2)}) collective-permute-start(f32[8,6,18,1]{2,0,3,1:T(8,128)S(1)} %copy.339), channel_id=1, source_target_pairs={{0,1},{2,3},{4,5},{6,7},{8,9},{10,11},{12,13},{14,15},{16,17},{18,... | collective-permute-start | bytes 10376 | tf_op jit(solution)/shard_map/ppermute | solution.py:25
  30.8 10.1 %add_add_fusion = f32[4,16,128]{2,1,0:T(8,128)S(1)} fusion(s32[4,16,128]{2,1,0:T(8,128)S(1)} %copy-done.3, f32[]{:T(128)} %bitcast.15, f32[]{:T(128)} %bitcast.14, f32[]{:T(128)} %bitcast.13, f32[]{:T(128)} %bitcast.12, f32[]{:T(128)} %bitcast.11, f32[]{:T(128)} %bitcast.10, f32[]{:T(128)} %bitcast.9, f32[]{:T(128)} %bitcast.8, f32[]{:T(128)} %bitcast.7, ...), kind=kLoop, calls=%fused_computation.217 | loop fusion | flops 393216 | bytes 65600 | tf_op jit(solution)/shard_map/add | solution.py:39
  43.5 4.3 %collective-permute-start.7 = (f32[8,1,16,128]{3,2,1,0:T(8,128)S(1)}, f32[8,1,16,128]{3,2,1,0:T(8,128)S(1)}, u32[]{:S(2)}, u32[]{:S(2)}) collective-permute-start(f32[8,1,16,128]{3,2,1,0:T(8,128)S(1)} %get-tuple-element.369), channel_id=1, source_target_pairs={{0,4},{4,8},{8,12},{12,16},{16,20},{20,24},{24,28},{1,5},{5,9},{9,... | collective-permute-start | bytes 196616 | tf_op jit(solution)/shard_map/ppermute | solution.py:25
  50.1 4.5 %collective-permute-start.9 = (f32[8,6,1,128]{3,0,2,1:T(8,128)S(1)}, f32[8,6,1,128]{3,0,2,1:T(8,128)S(1)}, u32[]{:S(2)}, u32[]{:S(2)}) collective-permute-start(f32[8,6,1,128]{3,0,2,1:T(8,128)S(1)} %copy.343), channel_id=1, source_target_pairs={{0,2},{1,3},{4,6},{5,7},{8,10},{9,11},{12,14},{13,15},{16,18},{17,... | collective-permute-start | bytes 73736 | tf_op jit(solution)/shard_map/ppermute | solution.py:25
  58.5 4.5 %collective-permute-start.11 = (f32[8,6,18,1]{2,0,3,1:T(8,128)S(1)}, f32[8,6,18,1]{2,0,3,1:T(8,128)S(1)}, u32[]{:S(2)}, u32[]{:S(2)}) collective-permute-start(f32[8,6,18,1]{2,0,3,1:T(8,128)S(1)} %copy.349), channel_id=1, source_target_pairs={{0,1},{2,3},{4,5},{6,7},{8,9},{10,11},{12,13},{14,15},{16,17},{18,... | collective-permute-start | bytes 10376 | tf_op jit(solution)/shard_map/ppermute | solution.py:25
  66.7 3.0 collective-permute-start.13
  72.0 4.5 %collective-permute-start.15 = (f32[8,6,1,128]{3,0,2,1:T(8,128)S(1)}, f32[8,6,1,128]{3,0,2,1:T(8,128)S(1)}, u32[]{:S(2)}, u32[]{:S(2)}) collective-permute-start(f32[8,6,1,128]{3,0,2,1:T(8,128)S(1)} %copy.353), channel_id=1, source_target_pairs={{0,2},{1,3},{4,6},{5,7},{8,10},{9,11},{12,14},{13,15},{16,18},{17,... | collective-permute-start | bytes 73736 | tf_op jit(solution)/shard_map/ppermute | solution.py:25
  80.5 4.5 %collective-permute-start.17 = (f32[8,6,18,1]{2,0,3,1:T(8,128)S(1)}, f32[8,6,18,1]{2,0,3,1:T(8,128)S(1)}, u32[]{:S(2)}, u32[]{:S(2)}) collective-permute-start(f32[8,6,18,1]{2,0,3,1:T(8,128)S(1)} %copy.359), channel_id=1, source_target_pairs={{0,1},{2,3},{4,5},{6,7},{8,9},{10,11},{12,13},{14,15},{16,17},{18,... | collective-permute-start | bytes 10376 | tf_op jit(solution)/shard_map/ppermute | solution.py:25
  85.0 32.8 %all_gather.13 = f32[4,2048]{1,0:T(4,128)S(1)} all-gather(f32[4,128]{1,0:T(4,128)S(1)} %copy-done.4), channel_id=1, replica_groups=mesh['row'=8,'col'=2,'gz'=2] {'row','gz'}, dimensions={1}, use_global_device_ids=true | all-gather | bytes 34816 | tf_op jit(solution)/shard_map/all_gather | solution.py:69
  117.8 4.6 %all_gather.14 = f32[4,256]{1,0:T(4,128)S(1)} all-gather(f32[4,128]{1,0:T(4,128)S(1)} %copy-done.4), channel_id=1, replica_groups=mesh['row'=8,'col'=2,'gz'=2] {'col'}, dimensions={1}, use_global_device_ids=true | all-gather | bytes 6144 | tf_op jit(solution)/shard_map/all_gather | solution.py:70
  123.7 2.6 copy.399
  127.6 3.0 collective-permute-start.19
  130.7 2.8 gather_fusion
  133.6 32.0 %all_gather.12 = bf16[8,2048]{0,1:T(8,128)(2,1)S(1)} all-gather(bf16[8,128]{0,1:T(8,128)(2,1)S(1)} %fusion.94), channel_id=1, replica_groups=mesh['row'=8,'col'=2,'gz'=2] {'row','gz'}, dimensions={1}, use_global_device_ids=true | all-gather | bytes 34816 | tf_op jit(solution)/shard_map/all_gather | solution.py:83
  167.2 4.5 %collective-permute-start.21 = (f32[8,6,1,128]{3,0,2,1:T(8,128)S(1)}, f32[8,6,1,128]{3,0,2,1:T(8,128)S(1)}, u32[]{:S(2)}, u32[]{:S(2)}) collective-permute-start(f32[8,6,1,128]{3,0,2,1:T(8,128)S(1)} %copy.367), channel_id=1, source_target_pairs={{0,2},{1,3},{4,6},{5,7},{8,10},{9,11},{12,14},{13,15},{16,18},{17,... | collective-permute-start | bytes 73736 | tf_op jit(solution)/shard_map/ppermute | solution.py:25
  171.7 9.6 %while.28 = (s32[]{:T(128)}, f32[8,256]{1,0:T(8,128)S(1)}, bf16[8,2048]{1,0:T(8,128)(2,1)S(1)}, f32[4,2048]{1,0:T(4,128)S(1)}, f32[4,256]{1,0:T(4,128)S(1)}, /*i...) while((s32[]{:T(128)}, f32[8,256]{1,0:T(8,128)S(1)}, ...), condition=%wide.region_1.3_spmd.clone, body=%wide.region_0.2_spmd.clone.sunk | while | flops 3936266 | bytes 58597 | solution.py:94
  184.7 4.5 %collective-permute-start.23 = (f32[8,6,18,1]{2,0,3,1:T(8,128)S(1)}, f32[8,6,18,1]{2,0,3,1:T(8,128)S(1)}, u32[]{:S(2)}, u32[]{:S(2)}) collective-permute-start(f32[8,6,18,1]{2,0,3,1:T(8,128)S(1)} %copy.373), channel_id=1, source_target_pairs={{0,1},{2,3},{4,5},{6,7},{8,9},{10,11},{12,13},{14,15},{16,17},{18,... | collective-permute-start | bytes 10376 | tf_op jit(solution)/shard_map/ppermute | solution.py:25
  190.0 3.6 %scatter_custom_fusion = f32[8,8192]{0,1:T(8,128)} fusion(s32[128]{0:T(128)S(1)} %compare_select_fusion, f32[]{:T(128)} %constant.128.clone.1, f32[8,128]{0,1:T(8,128)} %reduce-scatter.3.cloned.1.call-done, f32[]{:T(128)} %constant.147.clone.1, f32[128]{0:T(128)S(1)} %get-tuple-element.390), kind=kCustom, calls=%fused_computation.39 | custom fusion | flops 3072 | bytes 266760 | tf_op jit(solution)/shard_map/scatter-add | solution.py:101
  193.6 2.8 copy.400
  199.0 3.0 collective-permute-start.25
  204.3 4.5 %collective-permute-start.27 = (f32[8,6,1,128]{3,0,2,1:T(8,128)S(1)}, f32[8,6,1,128]{3,0,2,1:T(8,128)S(1)}, u32[]{:S(2)}, u32[]{:S(2)}) collective-permute-start(f32[8,6,1,128]{3,0,2,1:T(8,128)S(1)} %copy.377), channel_id=1, source_target_pairs={{0,2},{1,3},{4,6},{5,7},{8,10},{9,11},{12,14},{13,15},{16,18},{17,... | collective-permute-start | bytes 73736 | tf_op jit(solution)/shard_map/ppermute | solution.py:25
  212.8 4.5 %collective-permute-start.29 = (f32[8,6,18,1]{2,0,3,1:T(8,128)S(1)}, f32[8,6,18,1]{2,0,3,1:T(8,128)S(1)}, u32[]{:S(2)}, u32[]{:S(2)}) collective-permute-start(f32[8,6,18,1]{2,0,3,1:T(8,128)S(1)} %copy.383), channel_id=1, source_target_pairs={{0,1},{2,3},{4,5},{6,7},{8,9},{10,11},{12,13},{14,15},{16,17},{18,... | collective-permute-start | bytes 10376 | tf_op jit(solution)/shard_map/ppermute | solution.py:25
  220.9 3.0 collective-permute-start.31
  226.2 4.5 %collective-permute-start.33 = (f32[8,6,1,128]{3,0,2,1:T(8,128)S(1)}, f32[8,6,1,128]{3,0,2,1:T(8,128)S(1)}, u32[]{:S(2)}, u32[]{:S(2)}) collective-permute-start(f32[8,6,1,128]{3,0,2,1:T(8,128)S(1)} %copy.387), channel_id=1, source_target_pairs={{0,2},{1,3},{4,6},{5,7},{8,10},{9,11},{12,14},{13,15},{16,18},{17,... | collective-permute-start | bytes 73736 | tf_op jit(solution)/shard_map/ppermute | solution.py:25
  234.7 4.5 %collective-permute-start.35 = (f32[8,6,18,1]{2,0,3,1:T(8,128)S(1)}, f32[8,6,18,1]{2,0,3,1:T(8,128)S(1)}, u32[]{:S(2)}, u32[]{:S(2)}) collective-permute-start(f32[8,6,18,1]{2,0,3,1:T(8,128)S(1)} %copy.393), channel_id=1, source_target_pairs={{0,1},{2,3},{4,5},{6,7},{8,9},{10,11},{12,13},{14,15},{16,17},{18,... | collective-permute-start | bytes 10376 | tf_op jit(solution)/shard_map/ppermute | solution.py:25
  241.5 2.7 copy.401
  244.2 2.8 gather_fusion.1
  247.2 38.8 %all_gather.15 = bf16[8,2048]{0,1:T(8,128)(2,1)S(1)} all-gather(bf16[8,128]{0,1:T(8,128)(2,1)S(1)} %fusion.92), channel_id=1, replica_groups=mesh['row'=8,'col'=2,'gz'=2] {'row','gz'}, dimensions={1}, use_global_device_ids=true | all-gather | bytes 34816 | tf_op jit(solution)/shard_map/all_gather | solution.py:83
  286.2 9.7 %while.29 = (s32[]{:T(128)}, f32[8,256]{1,0:T(8,128)S(1)}, bf16[8,2048]{1,0:T(8,128)(2,1)S(1)}, f32[4,2048]{1,0:T(4,128)S(1)}, f32[4,256]{1,0:T(4,128)S(1)}, /*i...) while((s32[]{:T(128)}, f32[8,256]{1,0:T(8,128)S(1)}, ...), condition=%wide.region_5.7_spmd.clone, body=%wide.region_4.6_spmd.clone.sunk | while | flops 3936266 | bytes 58597 | solution.py:94
  296.6 7.8 %reduce-scatter.5.cloned.1.call-done = f32[8,128]{0,1:T(8,128)} async-done(((f32[8,256]{0,1:T(8,128)}), f32[8,128]{0,1:T(8,128)}) %reduce-scatter.5.cloned.1.call-update) | async-done | bytes 4112 | tf_op jit(solution)/shard_map/reduce_scatter | solution.py:95
  (190 shorter events, 79.6 us)
Async XLA Ops:
  7.2 182.8 %reduce-scatter.3.cloned.1.call-start = ((), (), s32[]{:S(2)}) async-start(), calls=%async_computation.2 | async-start | bytes 196608 | tf_op jit(solution)/shard_map/reduce_scatter | solution.py:95
  10.6 5.3 %collective-permute-start = (f32[8,1,16,128]{3,2,1,0:T(8,128)S(1)}, f32[8,1,16,128]{3,2,1,0:T(8,128)S(1)}, u32[]{:S(2)}, u32[]{:S(2)}) collective-permute-start(f32[8,1,16,128]{3,2,1,0:T(8,128)S(1)} %get-tuple-element.371), channel_id=1, source_target_pairs={{4,0},{8,4},{12,8},{16,12},{20,16},{24,20},{28,24},{5,1},{9,5},{13... | collective-permute-start | bytes 196616 | tf_op jit(solution)/shard_map/ppermute | solution.py:26
  16.0 7.8 %collective-permute-start.2 = (f32[8,6,1,128]{3,0,2,1:T(8,128)S(1)}, f32[8,6,1,128]{3,0,2,1:T(8,128)S(1)}, u32[]{:S(2)}, u32[]{:S(2)}) collective-permute-start(f32[8,6,1,128]{3,0,2,1:T(8,128)S(1)} %copy.402), channel_id=1, source_target_pairs={{2,0},{3,1},{6,4},{7,5},{10,8},{11,9},{14,12},{15,13},{18,16},{19,... | collective-permute-start | bytes 73736 | tf_op jit(solution)/shard_map/ppermute | solution.py:26
  17.3 6.6 %collective-permute-start.3 = (f32[8,6,1,128]{3,0,2,1:T(8,128)S(1)}, f32[8,6,1,128]{3,0,2,1:T(8,128)S(1)}, u32[]{:S(2)}, u32[]{:S(2)}) collective-permute-start(f32[8,6,1,128]{3,0,2,1:T(8,128)S(1)} %copy.403), channel_id=1, source_target_pairs={{0,2},{1,3},{4,6},{5,7},{8,10},{9,11},{12,14},{13,15},{16,18},{17,... | collective-permute-start | bytes 73736 | tf_op jit(solution)/shard_map/ppermute | solution.py:25
  24.6 16.3 %collective-permute-start.4 = (f32[8,6,18,1]{2,0,3,1:T(8,128)S(1)}, f32[8,6,18,1]{2,0,3,1:T(8,128)S(1)}, u32[]{:S(2)}, u32[]{:S(2)}) collective-permute-start(f32[8,6,18,1]{2,0,3,1:T(8,128)S(1)} %copy.337), channel_id=1, source_target_pairs={{1,0},{3,2},{5,4},{7,6},{9,8},{11,10},{13,12},{15,14},{17,16},{19,... | collective-permute-start | bytes 10376 | tf_op jit(solution)/shard_map/ppermute | solution.py:26
  26.3 15.1 %collective-permute-start.5 = (f32[8,6,18,1]{2,0,3,1:T(8,128)S(1)}, f32[8,6,18,1]{2,0,3,1:T(8,128)S(1)}, u32[]{:S(2)}, u32[]{:S(2)}) collective-permute-start(f32[8,6,18,1]{2,0,3,1:T(8,128)S(1)} %copy.339), channel_id=1, source_target_pairs={{0,1},{2,3},{4,5},{6,7},{8,9},{10,11},{12,13},{14,15},{16,17},{18,... | collective-permute-start | bytes 10376 | tf_op jit(solution)/shard_map/ppermute | solution.py:25
  42.2 5.7 %collective-permute-start.6 = (f32[8,1,16,128]{3,2,1,0:T(8,128)S(1)}, f32[8,1,16,128]{3,2,1,0:T(8,128)S(1)}, u32[]{:S(2)}, u32[]{:S(2)}) collective-permute-start(f32[8,1,16,128]{3,2,1,0:T(8,128)S(1)} %get-tuple-element.370), channel_id=1, source_target_pairs={{4,0},{8,4},{12,8},{16,12},{20,16},{24,20},{28,24},{5,1},{9,5},{13... | collective-permute-start | bytes 196616 | tf_op jit(solution)/shard_map/ppermute | solution.py:26
  43.5 5.2 %collective-permute-start.7 = (f32[8,1,16,128]{3,2,1,0:T(8,128)S(1)}, f32[8,1,16,128]{3,2,1,0:T(8,128)S(1)}, u32[]{:S(2)}, u32[]{:S(2)}) collective-permute-start(f32[8,1,16,128]{3,2,1,0:T(8,128)S(1)} %get-tuple-element.369), channel_id=1, source_target_pairs={{0,4},{4,8},{8,12},{12,16},{16,20},{20,24},{24,28},{1,5},{5,9},{9,... | collective-permute-start | bytes 196616 | tf_op jit(solution)/shard_map/ppermute | solution.py:25
  48.8 6.5 %collective-permute-start.8 = (f32[8,6,1,128]{3,0,2,1:T(8,128)S(1)}, f32[8,6,1,128]{3,0,2,1:T(8,128)S(1)}, u32[]{:S(2)}, u32[]{:S(2)}) collective-permute-start(f32[8,6,1,128]{3,0,2,1:T(8,128)S(1)} %copy.341), channel_id=1, source_target_pairs={{2,0},{3,1},{6,4},{7,5},{10,8},{11,9},{14,12},{15,13},{18,16},{19,... | collective-permute-start | bytes 73736 | tf_op jit(solution)/shard_map/ppermute | solution.py:26
  50.1 6.1 %collective-permute-start.9 = (f32[8,6,1,128]{3,0,2,1:T(8,128)S(1)}, f32[8,6,1,128]{3,0,2,1:T(8,128)S(1)}, u32[]{:S(2)}, u32[]{:S(2)}) collective-permute-start(f32[8,6,1,128]{3,0,2,1:T(8,128)S(1)} %copy.343), channel_id=1, source_target_pairs={{0,2},{1,3},{4,6},{5,7},{8,10},{9,11},{12,14},{13,15},{16,18},{17,... | collective-permute-start | bytes 73736 | tf_op jit(solution)/shard_map/ppermute | solution.py:25
  56.9 6.3 %collective-permute-start.10 = (f32[8,6,18,1]{2,0,3,1:T(8,128)S(1)}, f32[8,6,18,1]{2,0,3,1:T(8,128)S(1)}, u32[]{:S(2)}, u32[]{:S(2)}) collective-permute-start(f32[8,6,18,1]{2,0,3,1:T(8,128)S(1)} %copy.347), channel_id=1, source_target_pairs={{1,0},{3,2},{5,4},{7,6},{9,8},{11,10},{13,12},{15,14},{17,16},{19,... | collective-permute-start | bytes 10376 | tf_op jit(solution)/shard_map/ppermute | solution.py:26
  58.5 6.0 %collective-permute-start.11 = (f32[8,6,18,1]{2,0,3,1:T(8,128)S(1)}, f32[8,6,18,1]{2,0,3,1:T(8,128)S(1)}, u32[]{:S(2)}, u32[]{:S(2)}) collective-permute-start(f32[8,6,18,1]{2,0,3,1:T(8,128)S(1)} %copy.349), channel_id=1, source_target_pairs={{0,1},{2,3},{4,5},{6,7},{8,9},{10,11},{12,13},{14,15},{16,17},{18,... | collective-permute-start | bytes 10376 | tf_op jit(solution)/shard_map/ppermute | solution.py:25
  65.4 4.4 %collective-permute-start.12 = (f32[8,1,16,128]{3,2,1,0:T(8,128)S(1)}, f32[8,1,16,128]{3,2,1,0:T(8,128)S(1)}, u32[]{:S(2)}, u32[]{:S(2)}) collective-permute-start(f32[8,1,16,128]{3,2,1,0:T(8,128)S(1)} %get-tuple-element.368), channel_id=1, source_target_pairs={{4,0},{8,4},{12,8},{16,12},{20,16},{24,20},{28,24},{5,1},{9,5},{13... | collective-permute-start | bytes 196616 | tf_op jit(solution)/shard_map/ppermute | solution.py:26
  70.7 5.9 %collective-permute-start.14 = (f32[8,6,1,128]{3,0,2,1:T(8,128)S(1)}, f32[8,6,1,128]{3,0,2,1:T(8,128)S(1)}, u32[]{:S(2)}, u32[]{:S(2)}) collective-permute-start(f32[8,6,1,128]{3,0,2,1:T(8,128)S(1)} %copy.351), channel_id=1, source_target_pairs={{2,0},{3,1},{6,4},{7,5},{10,8},{11,9},{14,12},{15,13},{18,16},{19,... | collective-permute-start | bytes 73736 | tf_op jit(solution)/shard_map/ppermute | solution.py:26
  72.0 6.1 %collective-permute-start.15 = (f32[8,6,1,128]{3,0,2,1:T(8,128)S(1)}, f32[8,6,1,128]{3,0,2,1:T(8,128)S(1)}, u32[]{:S(2)}, u32[]{:S(2)}) collective-permute-start(f32[8,6,1,128]{3,0,2,1:T(8,128)S(1)} %copy.353), channel_id=1, source_target_pairs={{0,2},{1,3},{4,6},{5,7},{8,10},{9,11},{12,14},{13,15},{16,18},{17,... | collective-permute-start | bytes 73736 | tf_op jit(solution)/shard_map/ppermute | solution.py:25
  78.8 43.7 %collective-permute-start.16 = (f32[8,6,18,1]{2,0,3,1:T(8,128)S(1)}, f32[8,6,18,1]{2,0,3,1:T(8,128)S(1)}, u32[]{:S(2)}, u32[]{:S(2)}) collective-permute-start(f32[8,6,18,1]{2,0,3,1:T(8,128)S(1)} %copy.357), channel_id=1, source_target_pairs={{1,0},{3,2},{5,4},{7,6},{9,8},{11,10},{13,12},{15,14},{17,16},{19,... | collective-permute-start | bytes 10376 | tf_op jit(solution)/shard_map/ppermute | solution.py:26
  80.5 42.4 %collective-permute-start.17 = (f32[8,6,18,1]{2,0,3,1:T(8,128)S(1)}, f32[8,6,18,1]{2,0,3,1:T(8,128)S(1)}, u32[]{:S(2)}, u32[]{:S(2)}) collective-permute-start(f32[8,6,18,1]{2,0,3,1:T(8,128)S(1)} %copy.359), channel_id=1, source_target_pairs={{0,1},{2,3},{4,5},{6,7},{8,9},{10,11},{12,13},{14,15},{16,17},{18,... | collective-permute-start | bytes 10376 | tf_op jit(solution)/shard_map/ppermute | solution.py:25
  126.3 39.5 %collective-permute-start.18 = (f32[8,1,16,128]{3,2,1,0:T(8,128)S(1)}, f32[8,1,16,128]{3,2,1,0:T(8,128)S(1)}, u32[]{:S(2)}, u32[]{:S(2)}) collective-permute-start(f32[8,1,16,128]{3,2,1,0:T(8,128)S(1)} %get-tuple-element.366), channel_id=1, source_target_pairs={{4,0},{8,4},{12,8},{16,12},{20,16},{24,20},{28,24},{5,1},{9,5},{13... | collective-permute-start | bytes 196616 | tf_op jit(solution)/shard_map/ppermute | solution.py:26
  127.6 38.2 %collective-permute-start.19 = (f32[8,1,16,128]{3,2,1,0:T(8,128)S(1)}, f32[8,1,16,128]{3,2,1,0:T(8,128)S(1)}, u32[]{:S(2)}, u32[]{:S(2)}) collective-permute-start(f32[8,1,16,128]{3,2,1,0:T(8,128)S(1)} %get-tuple-element.365), channel_id=1, source_target_pairs={{0,4},{4,8},{8,12},{12,16},{16,20},{20,24},{24,28},{1,5},{5,9},{9,... | collective-permute-start | bytes 196616 | tf_op jit(solution)/shard_map/ppermute | solution.py:25
  165.9 16.4 %collective-permute-start.20 = (f32[8,6,1,128]{3,0,2,1:T(8,128)S(1)}, f32[8,6,1,128]{3,0,2,1:T(8,128)S(1)}, u32[]{:S(2)}, u32[]{:S(2)}) collective-permute-start(f32[8,6,1,128]{3,0,2,1:T(8,128)S(1)} %copy.365), channel_id=1, source_target_pairs={{2,0},{3,1},{6,4},{7,5},{10,8},{11,9},{14,12},{15,13},{18,16},{19,... | collective-permute-start | bytes 73736 | tf_op jit(solution)/shard_map/ppermute | solution.py:26
  167.2 15.1 %collective-permute-start.21 = (f32[8,6,1,128]{3,0,2,1:T(8,128)S(1)}, f32[8,6,1,128]{3,0,2,1:T(8,128)S(1)}, u32[]{:S(2)}, u32[]{:S(2)}) collective-permute-start(f32[8,6,1,128]{3,0,2,1:T(8,128)S(1)} %copy.367), channel_id=1, source_target_pairs={{0,2},{1,3},{4,6},{5,7},{8,10},{9,11},{12,14},{13,15},{16,18},{17,... | collective-permute-start | bytes 73736 | tf_op jit(solution)/shard_map/ppermute | solution.py:25
  182.2 122.3 %reduce-scatter.5.cloned.1.call-start = ((), (), s32[]{:S(2)}) async-start(), calls=%async_computation.3 | async-start | bytes 196608 | tf_op jit(solution)/shard_map/reduce_scatter | solution.py:95
  183.1 13.4 %collective-permute-start.22 = (f32[8,6,18,1]{2,0,3,1:T(8,128)S(1)}, f32[8,6,18,1]{2,0,3,1:T(8,128)S(1)}, u32[]{:S(2)}, u32[]{:S(2)}) collective-permute-start(f32[8,6,18,1]{2,0,3,1:T(8,128)S(1)} %copy.371), channel_id=1, source_target_pairs={{1,0},{3,2},{5,4},{7,6},{9,8},{11,10},{13,12},{15,14},{17,16},{19,... | collective-permute-start | bytes 10376 | tf_op jit(solution)/shard_map/ppermute | solution.py:26
  184.7 12.1 %collective-permute-start.23 = (f32[8,6,18,1]{2,0,3,1:T(8,128)S(1)}, f32[8,6,18,1]{2,0,3,1:T(8,128)S(1)}, u32[]{:S(2)}, u32[]{:S(2)}) collective-permute-start(f32[8,6,18,1]{2,0,3,1:T(8,128)S(1)} %copy.373), channel_id=1, source_target_pairs={{0,1},{2,3},{4,5},{6,7},{8,9},{10,11},{12,13},{14,15},{16,17},{18,... | collective-permute-start | bytes 10376 | tf_op jit(solution)/shard_map/ppermute | solution.py:25
  203.0 5.9 %collective-permute-start.26 = (f32[8,6,1,128]{3,0,2,1:T(8,128)S(1)}, f32[8,6,1,128]{3,0,2,1:T(8,128)S(1)}, u32[]{:S(2)}, u32[]{:S(2)}) collective-permute-start(f32[8,6,1,128]{3,0,2,1:T(8,128)S(1)} %copy.375), channel_id=1, source_target_pairs={{2,0},{3,1},{6,4},{7,5},{10,8},{11,9},{14,12},{15,13},{18,16},{19,... | collective-permute-start | bytes 73736 | tf_op jit(solution)/shard_map/ppermute | solution.py:26
  204.3 6.1 %collective-permute-start.27 = (f32[8,6,1,128]{3,0,2,1:T(8,128)S(1)}, f32[8,6,1,128]{3,0,2,1:T(8,128)S(1)}, u32[]{:S(2)}, u32[]{:S(2)}) collective-permute-start(f32[8,6,1,128]{3,0,2,1:T(8,128)S(1)} %copy.377), channel_id=1, source_target_pairs={{0,2},{1,3},{4,6},{5,7},{8,10},{9,11},{12,14},{13,15},{16,18},{17,... | collective-permute-start | bytes 73736 | tf_op jit(solution)/shard_map/ppermute | solution.py:25
  211.1 6.2 %collective-permute-start.28 = (f32[8,6,18,1]{2,0,3,1:T(8,128)S(1)}, f32[8,6,18,1]{2,0,3,1:T(8,128)S(1)}, u32[]{:S(2)}, u32[]{:S(2)}) collective-permute-start(f32[8,6,18,1]{2,0,3,1:T(8,128)S(1)} %copy.381), channel_id=1, source_target_pairs={{1,0},{3,2},{5,4},{7,6},{9,8},{11,10},{13,12},{15,14},{17,16},{19,... | collective-permute-start | bytes 10376 | tf_op jit(solution)/shard_map/ppermute | solution.py:26
  212.8 6.0 %collective-permute-start.29 = (f32[8,6,18,1]{2,0,3,1:T(8,128)S(1)}, f32[8,6,18,1]{2,0,3,1:T(8,128)S(1)}, u32[]{:S(2)}, u32[]{:S(2)}) collective-permute-start(f32[8,6,18,1]{2,0,3,1:T(8,128)S(1)} %copy.383), channel_id=1, source_target_pairs={{0,1},{2,3},{4,5},{6,7},{8,9},{10,11},{12,13},{14,15},{16,17},{18,... | collective-permute-start | bytes 10376 | tf_op jit(solution)/shard_map/ppermute | solution.py:25
  224.9 5.9 %collective-permute-start.32 = (f32[8,6,1,128]{3,0,2,1:T(8,128)S(1)}, f32[8,6,1,128]{3,0,2,1:T(8,128)S(1)}, u32[]{:S(2)}, u32[]{:S(2)}) collective-permute-start(f32[8,6,1,128]{3,0,2,1:T(8,128)S(1)} %copy.385), channel_id=1, source_target_pairs={{2,0},{3,1},{6,4},{7,5},{10,8},{11,9},{14,12},{15,13},{18,16},{19,... | collective-permute-start | bytes 73736 | tf_op jit(solution)/shard_map/ppermute | solution.py:26
  226.2 6.1 %collective-permute-start.33 = (f32[8,6,1,128]{3,0,2,1:T(8,128)S(1)}, f32[8,6,1,128]{3,0,2,1:T(8,128)S(1)}, u32[]{:S(2)}, u32[]{:S(2)}) collective-permute-start(f32[8,6,1,128]{3,0,2,1:T(8,128)S(1)} %copy.387), channel_id=1, source_target_pairs={{0,2},{1,3},{4,6},{5,7},{8,10},{9,11},{12,14},{13,15},{16,18},{17,... | collective-permute-start | bytes 73736 | tf_op jit(solution)/shard_map/ppermute | solution.py:25
  233.0 6.2 %collective-permute-start.34 = (f32[8,6,18,1]{2,0,3,1:T(8,128)S(1)}, f32[8,6,18,1]{2,0,3,1:T(8,128)S(1)}, u32[]{:S(2)}, u32[]{:S(2)}) collective-permute-start(f32[8,6,18,1]{2,0,3,1:T(8,128)S(1)} %copy.391), channel_id=1, source_target_pairs={{1,0},{3,2},{5,4},{7,6},{9,8},{11,10},{13,12},{15,14},{17,16},{19,... | collective-permute-start | bytes 10376 | tf_op jit(solution)/shard_map/ppermute | solution.py:26
  234.7 6.0 %collective-permute-start.35 = (f32[8,6,18,1]{2,0,3,1:T(8,128)S(1)}, f32[8,6,18,1]{2,0,3,1:T(8,128)S(1)}, u32[]{:S(2)}, u32[]{:S(2)}) collective-permute-start(f32[8,6,18,1]{2,0,3,1:T(8,128)S(1)} %copy.393), channel_id=1, source_target_pairs={{0,1},{2,3},{4,5},{6,7},{8,9},{10,11},{12,13},{14,15},{16,17},{18,... | collective-permute-start | bytes 10376 | tf_op jit(solution)/shard_map/ppermute | solution.py:25
  (12 other events, 204.4 us)
Sparse Core Ops, SparseCore 0:
  182.3 7.6 reduce-scatter.2
  296.8 7.6 reduce-scatter.4
where the time goes:
time: 314 us; the launch traced here: 313 us
  blocking collectives  108 us (34%)
  starting transfers between devices  96.7 us (31%)
  local copies, waits for them, and re-layouts  32.7 us (10%)
  waiting for transfers between devices  23.5 us (7%)
  matrix products  18.2 us (6%)
  other arithmetic  17.9 us (6%)
  between operations  15.6 us (5%)
    ppermute x18, starting transfers between devices, with_halo(): before = lax.ppermute(last, axis, up)  73.4 us
    all_gather x2, blocking collectives, local(): piece = lax.all_gather(density, ('row', 'gz'), axis=1, tiled=True)  70.8 us
    all_gather x1, blocking collectives, local(): lax.all_gather(panel_geometry, ('row', 'gz'), axis=1, tiled=True)  32.8 us
    ppermute x18, starting transfers between devices, with_halo(): after = lax.ppermute(initial, axis, down)  23.2 us
    dot_general x8, matrix products, add_block(): return carry + jnp.dot(values, tile, preferred_element_type=jnp.float32)  18.2 us
    ppermute x18, waiting for transfers between devices, with_halo(): before = lax.ppermute(last, axis, up)  11.8 us
    add x1, other arithmetic, relax(): diagonal = 6.0 + shift_field  10.1 us
    reduce_scatter x2, waiting for transfers between devices, local(): lax.psum_scatter(partial_value, 'col', scatter_dimension=1, tiled=True)  8.54 us
  transfers between devices with their start and end apart: 38, of which 14 were waited for; matrix products, arithmetic and copies ran while one was open for 12% of the time, Pallas kernels for 0%

commit v1 on v0

v1 whole, which is shorter than its diff:
```python
import functools
import math

import jax
import jax.numpy as jnp
import numpy as np
from jax import lax
from jax.experimental import pallas as pl
from jax.experimental.pallas import tpu as pltpu
from jax.sharding import PartitionSpec as P

SWEEPS = 3
ROUNDS = 2
STEPS = SWEEPS * ROUNDS

relax_weight = 0.8
wave_number = 25.0
soften = 0.05
coupling = 0.5

MESH = pl.DeviceIdType.MESH
AXES = ("row", "col", "gz")


def cosine_terms(degree=8):
    nodes = 0.125 * (1.0 + np.cos(np.pi * (np.arange(64) + 0.5) / 64))
    fitted = np.polynomial.Polynomial.fit(
        nodes, np.cos(2 * np.pi * np.sqrt(nodes)), degree, domain=[0.0, 0.25]
    )
    return [float(c) for c in fitted.convert().coef]


COSINE = cosine_terms()


def cosine_of_turns(turns):
    fraction = turns - jnp.floor(turns + 0.5)
    square = fraction * fraction
    value = jnp.full_like(square, COSINE[-1])
    for term in reversed(COSINE[:-1]):
        value = value * square + term
    return value


def kernel(
    sizes,
    init_hbm, source_hbm, class_hbm, shift_ref, cell_ref, live_ref, geo_ref,
    field_ref, potential_ref,
    init_v, source_v, class_v, weight_v, state_v, forcing_v,
    x_out, x_in, y_out, y_in, z_out, z_in,
    geo_all, column_v, tile_v, density_out, density_all,
    local_sem, face_send, face_recv, geo_sem, density_sem,
):
    rows, cols, depths = sizes
    devices = rows * cols * depths
    channels, size_x, size_y, size_z = init_hbm.shape
    slots = cell_ref.shape[1]
    classes = shift_ref.shape[0]
    factor = 1.0 / math.sqrt(slots * devices)
    here = tuple(lax.axis_index(axis) for axis in AXES)
    me = (here[0] * cols + here[1]) * depths + here[2]

    copies = [
        pltpu.make_async_copy(init_hbm, init_v, local_sem.at[0]),
        pltpu.make_async_copy(class_hbm, class_v, local_sem.at[1]),
        pltpu.make_async_copy(source_hbm, source_v, local_sem.at[2]),
    ]
    for copy in copies:
        copy.start()

    def each_other(action):
        def at(a, first):
            row = lax.rem(here[0] + a, rows)
            for b in range(cols):
                for c in range(depths):
                    if first and b == 0 and c == 0:
                        continue
                    action((row, lax.rem(here[1] + b, cols), lax.rem(here[2] + c, depths)))

        def others(i, carry):
            at(i, False)
            return carry

        lax.fori_loop(1, rows, others, 0)
        at(0, True)

    barrier = pltpu.get_barrier_semaphore()
    each_other(
        lambda device: pl.semaphore_signal(barrier, inc=1, device_id=device, device_id_type=MESH)
    )

    lane = lax.broadcasted_iota(jnp.int32, (size_y, size_z), 1)
    line = lax.broadcasted_iota(jnp.int32, (size_y, size_z), 0)
    half = size_z // 2

    def pack(k, e, x, value, packed):
        if x == 0:
            x_out[k, 0, e] = value.astype(x_out.dtype)
        if x == size_x - 1:
            x_out[k, 1, e] = value.astype(x_out.dtype)
        y_out[k, 0, e, x : x + 1, :] = value[0:1, :]
        y_out[k, 1, e, x : x + 1, :] = value[size_y - 1 : size_y, :]
        at = e * size_x + x
        low = jnp.broadcast_to(value[:, 0:1], value.shape)
        high = jnp.broadcast_to(value[:, size_z - 1 : size_z], value.shape)
        packed = jnp.where(lane == at, low, packed)
        return jnp.where(lane == at + half, high, packed)

    def face_copies(k):
        made = []
        for axis, (send, receive) in enumerate(((x_out, x_in), (y_out, y_in), (z_out, z_in))):
            count = sizes[axis]
            if count == 1:
                continue
            for up in (0, 1):
                target = {AXES[axis]: here[axis] + (1 if up else -1)}
                source = send.at[k] if axis == 2 else send.at[k, up]
                copy = pltpu.make_async_remote_copy(
                    src_ref=source,
                    dst_ref=receive.at[k, 1 - up],
                    send_sem=face_send.at[k, 2 * axis + up],
                    recv_sem=face_recv.at[k, 2 * axis + 1 - up],
                    device_id=target,
                    device_id_type=MESH,
                )
                sends = here[axis] < count - 1 if up else here[axis] > 0
                gets = here[axis] > 0 if up else here[axis] < count - 1
                made.append((copy, sends, gets))
        return made

    def start_faces(k):
        for copy, sends, _ in face_copies(k):
            pl.when(sends)(copy.start)

    def await_faces(k):
        for copy, _, gets in face_copies(k):
            pl.when(gets)(copy.wait_recv)

    def finish_faces(k):
        for copy, sends, _ in face_copies(k):
            pl.when(sends)(copy.wait_send)

    x_in[STEPS] = jnp.zeros(x_in.shape[1:], x_in.dtype)
    y_in[STEPS] = jnp.zeros(y_in.shape[1:], y_in.dtype)
    z_in[STEPS] = jnp.zeros(z_in.shape[1:], z_in.dtype)

    copies[0].wait()

    def pack_first(e, packed):
        for x in range(size_x):
            packed = pack(0, e, x, init_v[e, x], packed)
        return packed

    z_out[0] = lax.fori_loop(
        0, channels, pack_first, jnp.zeros((size_y, size_z), jnp.float32), unroll=True
    )

    eye = lax.broadcasted_iota(jnp.int32, (slots, slots), 0) == lax.broadcasted_iota(
        jnp.int32, (slots, slots), 1
    )
    for i in range(3):
        column = jnp.sum(jnp.where(eye, geo_ref[i : i + 1, :], 0.0), axis=1, keepdims=True)
        column_v[i] = jnp.broadcast_to(column, (slots, slots))
    geo_all[me] = geo_ref[...]

    pl.semaphore_wait(barrier, devices - 1)
    start_faces(0)

    def gather_copy(source, gathered, sems, device):
        return pltpu.make_async_remote_copy(
            src_ref=source,
            dst_ref=gathered.at[me],
            send_sem=sems.at[0],
            recv_sem=sems.at[1],
            device_id=device,
            device_id_type=MESH,
        )

    def start_gather(source, gathered, sems):
        each_other(lambda device: gather_copy(source, gathered, sems, device).start())

    def await_gather(gathered, sems, which):
        whole = gathered.at[pl.ds(0, devices - 1)]
        pltpu.make_async_copy(whole, whole, sems.at[which]).wait()

    start_gather(geo_ref, geo_all, geo_sem)

    copies[1].wait()
    for x in range(size_x):
        kind = class_v[x]
        shift = jnp.zeros(kind.shape, jnp.float32)
        for level in range(classes):
            shift = jnp.where(kind == level, shift_ref[level], shift)
        weight_v[x] = relax_weight / (6.0 + shift)

    cell = cell_ref[...]
    bits = size_z.bit_length() - 1
    cell_z = cell & (size_z - 1)
    cell_xy = cell >> bits
    pick_z = lax.broadcasted_iota(jnp.int32, (size_z, slots), 0) == cell_z
    pick_z = jnp.where(pick_z, 1.0, 0.0).astype(jnp.bfloat16)
    pick_xy = lax.broadcasted_iota(jnp.int32, (size_x * size_y, slots), 0) == cell_xy
    live = lax.broadcasted_iota(jnp.int32, (channels, slots), 1) < live_ref[0]
    which = lax.broadcasted_iota(jnp.int32, (channels, slots), 0)
    copies[2].wait()

    def sweep(k):
        now = (lambda e, x: init_v[e, x]) if k == 0 else (lambda e, x: state_v[k - 1, e, x])
        last = k == STEPS - 1
        force = source_v if k < SWEEPS else forcing_v
        slot = []
        for axis in range(3):
            below = jnp.where(here[axis] > 0, k, STEPS)
            above = jnp.where(here[axis] < sizes[axis] - 1, k, STEPS)
            slot.append((below, above))
        z_low, z_high = z_in[slot[2][0], 0], z_in[slot[2][1], 1]

        def body(e, packed):
            tiles = [now(e, x) for x in range(size_x)]
            before = x_in[slot[0][0], 0, e].astype(jnp.float32)
            after = x_in[slot[0][1], 1, e].astype(jnp.float32)
            spread = [before] + tiles + [after]
            for x in range(size_x):
                value = tiles[x]
                around = spread[x + 2] + spread[x]
                low = y_in[slot[1][0], 0, e, x : x + 1, :]
                high = y_in[slot[1][1], 1, e, x : x + 1, :]
                around = around + jnp.where(
                    line == size_y - 1, high, pltpu.roll(value, size_y - 1, 0)
                )
                around = around + jnp.where(line == 0, low, pltpu.roll(value, 1, 0))
                at = e * size_x + x
                high = pltpu.roll(z_high, lax.rem(2 * size_z - 1 - at, size_z), 1)
                low = pltpu.roll(z_low, lax.rem(size_z + half - at, size_z), 1)
                around = around + jnp.where(
                    lane == size_z - 1, high, pltpu.roll(value, size_z - 1, 1)
                )
                around = around + jnp.where(lane == 0, low, pltpu.roll(value, 1, 1))
                result = (1.0 - relax_weight) * value + weight_v[x] * (force[e, x] + around)
                if last:
                    field_ref[e, x] = result
                else:
                    state_v[k, e, x] = result
                    packed = pack(k + 1, e, x, result, packed)
            return packed

        packed = lax.fori_loop(
            0, channels, body, jnp.zeros((size_y, size_z), jnp.float32), unroll=2
        )
        if not last:
            z_out[k + 1] = packed

    pieces = 4
    chunk = slots // pieces

    def make_tiles(first, stop):
        def body(s, carry):
            source = geo_all[s]
            for piece in range(pieces):
                span = slice(piece * chunk, (piece + 1) * chunk)
                delta_x = column_v[0, span, :] - source[0:1, :]
                delta_y = column_v[1, span, :] - source[1:2, :]
                delta_z = column_v[2, span, :] - source[2:3, :]
                distance = jnp.sqrt(delta_x * delta_x + delta_y * delta_y + delta_z * delta_z)
                wave = cosine_of_turns(distance * (wave_number / (2.0 * math.pi)))
                value = (source[3:4, :] * factor) * wave / (distance + soften)
                tile_v[s, span, :] = value.astype(tile_v.dtype)
            return carry

        lax.fori_loop(first, stop, body, 0)

    group = math.gcd(devices, 8)

    def apply_tiles(gathered):
        def body(i, total):
            for j in range(group):
                s = i * group + j
                total = total + lax.dot_general(
                    gathered[s], tile_v[s], (((1,), (1,)), ((), ())),
                    preferred_element_type=jnp.float32,
                )
            return total

        return lax.fori_loop(
            0, devices // group, body, jnp.zeros((channels, slots), jnp.float32)
        )

    cut = [0, 3 * devices // 8, 3 * devices // 4, devices]
    for k in range(STEPS):
        if k == 1:
            await_gather(geo_all, geo_sem, 1)
        if k in (1, 2):
            make_tiles(cut[k - 1], cut[k])
        await_faces(k)
        sweep(k)
        end = k % SWEEPS == SWEEPS - 1
        if k + 1 < STEPS:
            start_faces(k + 1)
        if not end:
            continue
        r = k // SWEEPS
        ending = field_ref if k == STEPS - 1 else state_v.at[k]
        flat = ending[...].reshape(channels * size_x * size_y, size_z).astype(jnp.bfloat16)
        picked = jnp.dot(flat, pick_z, preferred_element_type=jnp.float32)
        density = jnp.zeros((channels, slots), jnp.float32)
        for e in range(channels):
            block = picked[e * size_x * size_y : (e + 1) * size_x * size_y]
            found = jnp.sum(jnp.where(pick_xy, block, 0.0), axis=0, keepdims=True)
            density = jnp.where(which == e, found, density)
        density = jnp.where(live, density, 0.0).astype(jnp.bfloat16)
        density_out[r] = density
        density_all[r, me] = density
        start_gather(density_out.at[r], density_all.at[r], density_sem.at[r])
        if r == 0:
            make_tiles(cut[2], cut[3])
        await_gather(density_all.at[r], density_sem.at[r], 1)
        potential = jnp.where(live, apply_tiles(density_all.at[r]), 0.0)
        if r == ROUNDS - 1:
            potential_ref[...] = potential
        else:
            half_of = coupling * potential
            big = half_of.astype(jnp.bfloat16).astype(jnp.float32)
            small = half_of - big
            for e in range(channels):
                load = jnp.zeros((size_x * size_y, size_z), jnp.float32)
                for part in (big, small):
                    placed = jnp.where(pick_xy, part[e : e + 1, :], 0.0).astype(jnp.bfloat16)
                    load = load + lax.dot_general(
                        placed, pick_z, (((1,), (1,)), ((), ())),
                        preferred_element_type=jnp.float32,
                    )
                forcing_v[e] = source_v[e] + load.reshape(size_x, size_y, size_z)

    for k in range(STEPS):
        finish_faces(k)
    await_gather(geo_all, geo_sem, 0)
    for r in range(ROUNDS):
        await_gather(density_all.at[r], density_sem.at[r], 0)


def local(sizes, initial_field, source_term, cell_class, class_shift, surface_cell, live_count,
          panel_geometry):
    channels, size_x, size_y, size_z = initial_field.shape
    slots = surface_cell.shape[0]
    devices = sizes[0] * sizes[1] * sizes[2]
    brick = (channels, size_x, size_y, size_z)
    vmem = pl.BlockSpec(memory_space=pltpu.VMEM)
    smem = pl.BlockSpec(memory_space=pltpu.SMEM)
    hbm = pl.BlockSpec(memory_space=pl.ANY)
    return pl.pallas_call(
        functools.partial(kernel, sizes),
        out_shape=(
            jax.ShapeDtypeStruct(brick, jnp.float32),
            jax.ShapeDtypeStruct((channels, slots), jnp.float32),
        ),
        in_specs=[hbm, hbm, hbm, smem, vmem, smem, vmem],
        out_specs=(vmem, vmem),
        scratch_shapes=[
            pltpu.VMEM(brick, jnp.float32),
            pltpu.VMEM(brick, jnp.float32),
            pltpu.VMEM(brick[1:], jnp.int32),
            pltpu.VMEM(brick[1:], jnp.float32),
            pltpu.VMEM((STEPS - 1,) + brick, jnp.float32),
            pltpu.VMEM(brick, jnp.float32),
            pltpu.VMEM((STEPS, 2, channels, size_y, size_z), jnp.bfloat16),
            pltpu.VMEM((STEPS + 1, 2, channels, size_y, size_z), jnp.bfloat16),
            pltpu.VMEM((STEPS, 2, channels, size_x, size_z), jnp.float32),
            pltpu.VMEM((STEPS + 1, 2, channels, size_x, size_z), jnp.float32),
            pltpu.VMEM((STEPS, size_y, size_z), jnp.float32),
            pltpu.VMEM((STEPS + 1, 2, size_y, size_z), jnp.float32),
            pltpu.VMEM((devices, 4, slots), jnp.float32),
            pltpu.VMEM((3, slots, slots), jnp.float32),
            pltpu.VMEM((devices, slots, slots), jnp.bfloat16),
            pltpu.VMEM((ROUNDS, channels, slots), jnp.bfloat16),
            pltpu.VMEM((ROUNDS, devices, channels, slots), jnp.bfloat16),
            pltpu.SemaphoreType.DMA((3,)),
            pltpu.SemaphoreType.DMA((STEPS, 6)),
            pltpu.SemaphoreType.DMA((STEPS, 6)),
            pltpu.SemaphoreType.DMA((2,)),
            pltpu.SemaphoreType.DMA((ROUNDS, 2)),
        ],
        compiler_params=pltpu.CompilerParams(
            collective_id=0, has_side_effects=True, vmem_limit_bytes=60 * 1024 * 1024
        ),
    )(
        initial_field, source_term, cell_class, class_shift,
        surface_cell.reshape(1, slots), live_count, panel_geometry,
    )


def solution(mesh):
    placed = (
        P(None, "row", "col", "gz"),
        P(None, "row", "col", "gz"),
        P("row", "col", "gz"),
        P(),
        P(("row", "col", "gz")),
        P(("row", "col", "gz")),
        P(None, ("row", "col", "gz")),
    )
    return jax.shard_map(
        functools.partial(local, tuple(mesh.shape[axis] for axis in AXES)),
        mesh=mesh,
        in_specs=placed,
        out_specs=(P(None, "row", "col", "gz"), P(None, ("row", "col", "gz"))),
        check_vma=False,
    )
```

time: 314 us -> 44.4 us (0.14)
  blocking collectives: 108 us -> 0 us
  starting transfers between devices: 96.7 us -> 0 us
  Pallas kernels: 0 us -> 40.6 us
  local copies, waits for them, and re-layouts: 32.7 us -> 2.27 us
  waiting for transfers between devices: 23.5 us -> 0 us
  matrix products: 18.2 us -> 0 us
  other arithmetic: 17.9 us -> 0 us
  between operations: 15.6 us -> 1.29 us
    all_gather x4 -> x0, blocking collectives: 108 us -> none  [the longest x2 70.8 us: local(): piece = lax.all_gather(density, ('row', 'gz'), axis=1, tiled=True)]
    ppermute x36 -> x0, starting transfers between devices: 96.6 us -> none  [the longest x18 73.4 us: with_halo(): before = lax.ppermute(last, axis, up)]
    pallas_call x0 -> x1, Pallas kernels: none -> 40.6 us  [local(): pl.pallas_call(functools.partial(kernel, sizes), out_shape=(jax.ShapeDtyp...]
    dot_general x8 -> x0, matrix products: 18.2 us -> none  [add_block(): return carry + jnp.dot(values, tile, preferred_element_type=jnp.float32)]
    ppermute x36 -> x0, waiting for transfers between devices: 14.9 us -> none  [the longest x18 11.8 us: with_halo(): before = lax.ppermute(last, axis, up)]
    add x7 -> x0, other arithmetic: 12.4 us -> none  [the longest x1 10.1 us: relax(): diagonal = 6.0 + shift_field]
    slice x52 -> x0, local copies, waits for them, and re-layouts: 9.96 us -> none  [the longest x18 4.58 us: with_halo(): initial = lax.slice_in_dim(x, 0, width, axis=dim)]
    reduce_scatter x2 -> x0, waiting for transfers between devices: 8.54 us -> none  [local(): lax.psum_scatter(partial_value, 'col', scatter_dimension=1, tiled=True)]
  transfers between devices with their start and end apart: 38 -> 0, of which waited for: 14 -> 0; matrix products, arithmetic and copies ran while one was open for 12% -> 0% of each run, Pallas kernels for 0% -> 0%
where the time goes in v1:
time: 44.4 us; the launch traced here: 44.2 us
  Pallas kernels  40.6 us (91%)
  local copies, waits for them, and re-layouts  2.27 us (5%)
  between operations  1.29 us (3%)
    pallas_call x1, Pallas kernels, local(): pl.pallas_call(functools.partial(kernel, sizes), out_shape=(jax.ShapeDtyp...  40.6 us
    unnamed x4, local copies, waits for them, and re-layouts  2.27 us

profile of v1, /device:TPU:0, one launch (start us, length us, event | category | flops | bytes accessed | tf_op | source)
XLA Modules:
  0.0 44.2 jit_solution(12672680676155733304)
XLA Ops:
  1.3 40.6 %shard_map.86 = (f32[8,4,16,128]{3,2,1,0:T(8,128)}, f32[8,128]{1,0:T(8,128)}) custom-call(f32[8,4,16,128]{3,2,1,0:T(8,128)} %init_hbm.1, f32[8,4,16,128]{3,2,1,0:T(8,128)} %source_hbm.1, s32[4,16,128]{2,1,0:T(8,128)} %class_hbm.1, f32[16]{0:T(128)} %shift_ref.1, s32[1,128]{1,0:T(1,128)} %bitcast.1, s32[1]{0:T(128)S(6)} %copy.11.live_ref, f32[4,128]{1,0:T(4,128)} %geo_ref.1), custom_call_target="tpu_custom_call" | custom-call | tf_op jit(solution)/shard_map/pallas_call | solution.py:350
  41.9 0.0 copy-start
  41.9 1.7 %copy.12 = f32[8,4,16,128]{3,2,1,0:T(8,128)} copy(f32[8,4,16,128]{3,2,1,0:T(8,128)} %get-tuple-element.4) | data formatting | bytes 524288
  43.6 0.0 copy-done
  43.6 0.6 %copy.13 = f32[8,128]{1,0:T(8,128)} copy(f32[8,128]{1,0:T(8,128)S(1)} %copy-done) | data formatting | bytes 8192
Async XLA Ops:
  41.9 1.7 %copy-start = (f32[8,128]{1,0:T(8,128)S(1)}, f32[8,128]{1,0:T(8,128)}, u32[]{:S(2)}) copy-start(f32[8,128]{1,0:T(8,128)} %get-tuple-element.5) | copy-start | bytes 12292

commit v2 on v1

--- a/solution.py
+++ b/solution.py
@@ -44,17 +44,18 @@
 
 def kernel(
     sizes,
-    init_hbm, source_hbm, class_hbm, shift_ref, cell_ref, live_ref, geo_ref,
+    init_hbm, source_hbm, class_hbm, shift_hbm, cell_hbm, geo_hbm, live_ref,
     field_ref, potential_ref,
     init_v, source_v, class_v, weight_v, state_v, forcing_v,
     x_out, x_in, y_out, y_in, z_out, z_in,
     geo_all, column_v, tile_v, density_out, density_all,
+    shift_ref, cell_ref, geo_ref,
     local_sem, face_send, face_recv, geo_sem, density_sem,
 ):
     rows, cols, depths = sizes
     devices = rows * cols * depths
     channels, size_x, size_y, size_z = init_hbm.shape
-    slots = cell_ref.shape[1]
+    slots = cell_hbm.shape[1]
     classes = shift_ref.shape[0]
     factor = 1.0 / math.sqrt(slots * devices)
     here = tuple(lax.axis_index(axis) for axis in AXES)
@@ -64,6 +65,9 @@
         pltpu.make_async_copy(init_hbm, init_v, local_sem.at[0]),
         pltpu.make_async_copy(class_hbm, class_v, local_sem.at[1]),
         pltpu.make_async_copy(source_hbm, source_v, local_sem.at[2]),
+        pltpu.make_async_copy(geo_hbm, geo_ref, local_sem.at[3]),
+        pltpu.make_async_copy(shift_hbm, shift_ref, local_sem.at[4]),
+        pltpu.make_async_copy(cell_hbm, cell_ref, local_sem.at[5]),
     ]
     for copy in copies:
         copy.start()
@@ -91,7 +95,8 @@
 
     lane = lax.broadcasted_iota(jnp.int32, (size_y, size_z), 1)
     line = lax.broadcasted_iota(jnp.int32, (size_y, size_z), 0)
-    half = size_z // 2
+    pair = lane >> 1
+    edge = (lane == 0) | (lane == size_z - 1)
 
     def pack(k, e, x, value, packed):
         if x == 0:
@@ -101,10 +106,7 @@
         y_out[k, 0, e, x : x + 1, :] = value[0:1, :]
         y_out[k, 1, e, x : x + 1, :] = value[size_y - 1 : size_y, :]
         at = e * size_x + x
-        low = jnp.broadcast_to(value[:, 0:1], value.shape)
-        high = jnp.broadcast_to(value[:, size_z - 1 : size_z], value.shape)
-        packed = jnp.where(lane == at, low, packed)
-        return jnp.where(lane == at + half, high, packed)
+        return jnp.where(pair == at, pltpu.roll(value, lax.rem(2 * at + 1, size_z), 1), packed)
 
     def face_copies(k):
         made = []
@@ -155,6 +157,7 @@
         0, channels, pack_first, jnp.zeros((size_y, size_z), jnp.float32), unroll=True
     )
 
+    copies[3].wait()
     eye = lax.broadcasted_iota(jnp.int32, (slots, slots), 0) == lax.broadcasted_iota(
         jnp.int32, (slots, slots), 1
     )
@@ -186,6 +189,7 @@
     start_gather(geo_ref, geo_all, geo_sem)
 
     copies[1].wait()
+    copies[4].wait()
     for x in range(size_x):
         kind = class_v[x]
         shift = jnp.zeros(kind.shape, jnp.float32)
@@ -193,6 +197,7 @@
             shift = jnp.where(kind == level, shift_ref[level], shift)
         weight_v[x] = relax_weight / (6.0 + shift)
 
+    copies[5].wait()
     cell = cell_ref[...]
     bits = size_z.bit_length() - 1
     cell_z = cell & (size_z - 1)
@@ -204,39 +209,61 @@
     which = lax.broadcasted_iota(jnp.int32, (channels, slots), 0)
     copies[2].wait()
 
-    def sweep(k):
-        now = (lambda e, x: init_v[e, x]) if k == 0 else (lambda e, x: state_v[k - 1, e, x])
+    def now(k, e, x):
+        return init_v[e, x] if k == 0 else state_v[k - 1, e, x]
+
+    def inner(k):
+        force = source_v if k <= SWEEPS else forcing_v
+
+        def body(e, carry):
+            tiles = [now(k, e, x) for x in range(size_x)]
+            for x in range(size_x):
+                value = tiles[x]
+                around = force[e, x]
+                if x + 1 < size_x:
+                    around = around + tiles[x + 1]
+                if x > 0:
+                    around = around + tiles[x - 1]
+                around = around + jnp.where(
+                    line == size_y - 1, 0.0, pltpu.roll(value, size_y - 1, 0)
+                )
+                around = around + jnp.where(line == 0, 0.0, pltpu.roll(value, 1, 0))
+                around = around + jnp.where(
+                    lane == size_z - 1, 0.0, pltpu.roll(value, size_z - 1, 1)
+                )
+                around = around + jnp.where(lane == 0, 0.0, pltpu.roll(value, 1, 1))
+                state_v[k, e, x] = (1.0 - relax_weight) * value + weight_v[x] * around
+            return carry
+
+        lax.fori_loop(0, channels, body, 0, unroll=8)
+
+    def outer(k):
         last = k == STEPS - 1
-        force = source_v if k < SWEEPS else forcing_v
         slot = []
         for axis in range(3):
             below = jnp.where(here[axis] > 0, k, STEPS)
             above = jnp.where(here[axis] < sizes[axis] - 1, k, STEPS)
             slot.append((below, above))
-        z_low, z_high = z_in[slot[2][0], 0], z_in[slot[2][1], 1]
+        beyond = jnp.where(
+            (lane & 1) == 0, z_in[slot[2][0], 0], pltpu.roll(z_in[slot[2][1], 1], size_z - 2, 1)
+        )
 
         def body(e, packed):
-            tiles = [now(e, x) for x in range(size_x)]
-            before = x_in[slot[0][0], 0, e].astype(jnp.float32)
-            after = x_in[slot[0][1], 1, e].astype(jnp.float32)
-            spread = [before] + tiles + [after]
             for x in range(size_x):
-                value = tiles[x]
-                around = spread[x + 2] + spread[x]
                 low = y_in[slot[1][0], 0, e, x : x + 1, :]
                 high = y_in[slot[1][1], 1, e, x : x + 1, :]
+                at = e * size_x + x
+                around = jnp.where(
+                    edge, pltpu.roll(beyond, lax.rem(2 * size_z - 2 * at, size_z), 1), 0.0
+                )
                 around = around + jnp.where(
-                    line == size_y - 1, high, pltpu.roll(value, size_y - 1, 0)
+                    line == 0, low, jnp.where(line == size_y - 1, high, 0.0)
                 )
-                around = around + jnp.where(line == 0, low, pltpu.roll(value, 1, 0))
-                at = e * size_x + x
-                high = pltpu.roll(z_high, lax.rem(2 * size_z - 1 - at, size_z), 1)
-                low = pltpu.roll(z_low, lax.rem(size_z + half - at, size_z), 1)
-                around = around + jnp.where(
-                    lane == size_z - 1, high, pltpu.roll(value, size_z - 1, 1)
-                )
-                around = around + jnp.where(lane == 0, low, pltpu.roll(value, 1, 1))
-                result = (1.0 - relax_weight) * value + weight_v[x] * (force[e, x] + around)
+                if x == 0:
+                    around = around + x_in[slot[0][0], 0, e].astype(jnp.float32)
+                if x == size_x - 1:
+                    around = around + x_in[slot[0][1], 1, e].astype(jnp.float32)
+                result = state_v[k, e, x] + weight_v[x] * around
                 if last:
                     field_ref[e, x] = result
                 else:
@@ -245,7 +272,7 @@
             return packed
 
         packed = lax.fori_loop(
-            0, channels, body, jnp.zeros((size_y, size_z), jnp.float32), unroll=2
+            0, channels, body, jnp.zeros((size_y, size_z), jnp.float32), unroll=8
         )
         if not last:
             z_out[k + 1] = packed
@@ -256,6 +283,7 @@
     def make_tiles(first, stop):
         def body(s, carry):
             source = geo_all[s]
+            values = []
             for piece in range(pieces):
                 span = slice(piece * chunk, (piece + 1) * chunk)
                 delta_x = column_v[0, span, :] - source[0:1, :]
@@ -264,7 +292,9 @@
                 distance = jnp.sqrt(delta_x * delta_x + delta_y * delta_y + delta_z * delta_z)
                 wave = cosine_of_turns(distance * (wave_number / (2.0 * math.pi)))
                 value = (source[3:4, :] * factor) * wave / (distance + soften)
-                tile_v[s, span, :] = value.astype(tile_v.dtype)
+                values.append(value)
+            turned = jnp.concatenate(values, axis=0).T
+            tile_v[pl.ds(pl.multiple_of(s * slots, slots), slots), :] = turned.astype(tile_v.dtype)
             return carry
 
         lax.fori_loop(first, stop, body, 0)
@@ -273,26 +303,24 @@
 
     def apply_tiles(gathered):
         def body(i, total):
-            for j in range(group):
-                s = i * group + j
-                total = total + lax.dot_general(
-                    gathered[s], tile_v[s], (((1,), (1,)), ((), ())),
-                    preferred_element_type=jnp.float32,
-                )
-            return total
+            values = jnp.concatenate([gathered[i * group + j] for j in range(group)], axis=1)
+            span = pl.ds(pl.multiple_of(i * group * slots, group * slots), group * slots)
+            return total + jnp.dot(values, tile_v[span, :], preferred_element_type=jnp.float32)
 
         return lax.fori_loop(
             0, devices // group, body, jnp.zeros((channels, slots), jnp.float32)
         )
 
-    cut = [0, 3 * devices // 8, 3 * devices // 4, devices]
+    cut = [0, devices // 4, devices // 2, devices]
     for k in range(STEPS):
+        if k != SWEEPS:
+            inner(k)
         if k == 1:
             await_gather(geo_all, geo_sem, 1)
         if k in (1, 2):
             make_tiles(cut[k - 1], cut[k])
         await_faces(k)
-        sweep(k)
+        outer(k)
         end = k % SWEEPS == SWEEPS - 1
         if k + 1 < STEPS:
             start_faces(k + 1)
@@ -311,6 +339,8 @@
         density_out[r] = density
         density_all[r, me] = density
         start_gather(density_out.at[r], density_all.at[r], density_sem.at[r])
+        if r < ROUNDS - 1:
+            inner(k + 1)
         if r == 0:
             make_tiles(cut[2], cut[3])
         await_gather(density_all.at[r], density_sem.at[r], 1)
@@ -329,7 +359,9 @@
                         placed, pick_z, (((1,), (1,)), ((), ())),
                         preferred_element_type=jnp.float32,
                     )
-                forcing_v[e] = source_v[e] + load.reshape(size_x, size_y, size_z)
+                load = load.reshape(size_x, size_y, size_z)
+                forcing_v[e] = source_v[e] + load
+                state_v[k + 1, e] = state_v[k + 1, e] + weight_v[...] * load
 
     for k in range(STEPS):
         finish_faces(k)
@@ -345,22 +377,31 @@
     devices = sizes[0] * sizes[1] * sizes[2]
     brick = (channels, size_x, size_y, size_z)
     vmem = pl.BlockSpec(memory_space=pltpu.VMEM)
-    smem = pl.BlockSpec(memory_space=pltpu.SMEM)
-    hbm = pl.BlockSpec(memory_space=pl.ANY)
+    hbm = pl.BlockSpec(memory_space=pltpu.HBM)
+    per_device = slots * (2 * slots + 4 * 8 + ROUNDS * 2 * channels)
+    grant = devices * per_device + 24 * 4 * math.prod(brick)
+    operands = [
+        pltpu.with_memory_space_constraint(array, pltpu.HBM)
+        for array in (
+            initial_field, source_term, cell_class, class_shift,
+            surface_cell.reshape(1, slots), panel_geometry,
+        )
+    ]
+    operands.append(live_count)
     return pl.pallas_call(
         functools.partial(kernel, sizes),
         out_shape=(
             jax.ShapeDtypeStruct(brick, jnp.float32),
             jax.ShapeDtypeStruct((channels, slots), jnp.float32),
         ),
-        in_specs=[hbm, hbm, hbm, smem, vmem, smem, vmem],
+        in_specs=[hbm] * 6 + [pl.BlockSpec(memory_space=pltpu.SMEM)],
         out_specs=(vmem, vmem),
         scratch_shapes=[
             pltpu.VMEM(brick, jnp.float32),
             pltpu.VMEM(brick, jnp.float32),
             pltpu.VMEM(brick[1:], jnp.int32),
             pltpu.VMEM(brick[1:], jnp.float32),
-            pltpu.VMEM((STEPS - 1,) + brick, jnp.float32),
+            pltpu.VMEM((STEPS,) + brick, jnp.float32),
             pltpu.VMEM(brick, jnp.float32),
             pltpu.VMEM((STEPS, 2, channels, size_y, size_z), jnp.bfloat16),
             pltpu.VMEM((STEPS + 1, 2, channels, size_y, size_z), jnp.bfloat16),
@@ -370,22 +411,22 @@
             pltpu.VMEM((STEPS + 1, 2, size_y, size_z), jnp.float32),
             pltpu.VMEM((devices, 4, slots), jnp.float32),
             pltpu.VMEM((3, slots, slots), jnp.float32),
-            pltpu.VMEM((devices, slots, slots), jnp.bfloat16),
+            pltpu.VMEM((devices * slots, slots), jnp.bfloat16),
             pltpu.VMEM((ROUNDS, channels, slots), jnp.bfloat16),
             pltpu.VMEM((ROUNDS, devices, channels, slots), jnp.bfloat16),
-            pltpu.SemaphoreType.DMA((3,)),
+            pltpu.SMEM(class_shift.shape, jnp.float32),
+            pltpu.VMEM((1, slots), jnp.int32),
+            pltpu.VMEM(panel_geometry.shape, jnp.float32),
+            pltpu.SemaphoreType.DMA((6,)),
             pltpu.SemaphoreType.DMA((STEPS, 6)),
             pltpu.SemaphoreType.DMA((STEPS, 6)),
             pltpu.SemaphoreType.DMA((2,)),
             pltpu.SemaphoreType.DMA((ROUNDS, 2)),
         ],
         compiler_params=pltpu.CompilerParams(
-            collective_id=0, has_side_effects=True, vmem_limit_bytes=60 * 1024 * 1024
+            collective_id=0, has_side_effects=True, vmem_limit_bytes=grant
         ),
-    )(
-        initial_field, source_term, cell_class, class_shift,
-        surface_cell.reshape(1, slots), live_count, panel_geometry,
-    )
+    )(*operands)
 
 
 def solution(mesh):

time: 44.4 us -> 37.2 us (0.84)
  Pallas kernels: 40.6 us -> 34.5 us
  local copies, waits for them, and re-layouts: 2.27 us -> 1.3 us
    pallas_call x1, Pallas kernels: 40.6 us -> 34.5 us  [local(): pl.pallas_call(functools.partial(kernel, sizes), out_shape=(jax.ShapeDtyp...]
    unnamed x4 -> x2, local copies, waits for them, and re-layouts: 2.27 us -> 1.3 us
where the time goes in v2:
time: 37.2 us; the launch traced here: 37 us
  Pallas kernels  34.5 us (93%)
  local copies, waits for them, and re-layouts  1.3 us (3%)
  between operations  1.29 us (3%)
    pallas_call x1, Pallas kernels, local(): pl.pallas_call(functools.partial(kernel, sizes), out_shape=(jax.ShapeDtyp...  34.5 us
    unnamed x2, local copies, waits for them, and re-layouts  1.3 us

profile of v2, /device:TPU:0, one launch (start us, length us, event | category | flops | bytes accessed | tf_op | source)
XLA Modules:
  0.0 37.0 jit_solution(1488213874003501266)
XLA Ops:
  1.3 34.5 %shard_map.86 = (f32[8,4,16,128]{3,2,1,0:T(8,128)S(1)}, f32[8,128]{1,0:T(8,128)S(1)}) custom-call(f32[8,4,16,128]{3,2,1,0:T(8,128)} %init_hbm.1, f32[8,4,16,128]{3,2,1,0:T(8,128)} %source_hbm.1, s32[4,16,128]{2,1,0:T(8,128)} %class_hbm.1, f32[16]{0:T(128)} %shift_hbm.1, s32[1,128]{1,0:T(1,128)} %bitcast.1, f32[4,128]{1,0:T(4,128)} %geo_hbm.1, ...), custom_call_target="tpu_custom_call" | custom-call | tf_op jit(solution)/shard_map/pallas_call | solution.py:391
  35.7 0.7 %copy.12 = f32[8,4,16,128]{3,2,1,0:T(8,128)} copy(f32[8,4,16,128]{3,2,1,0:T(8,128)S(1)} %get-tuple-element.4) | data formatting | bytes 524288
  36.4 0.6 %copy.13 = f32[8,128]{1,0:T(8,128)} copy(f32[8,128]{1,0:T(8,128)S(1)} %get-tuple-element.5) | data formatting | bytes 8192
